TPU v7x, 512 devices: a 8x2x16 block of a 8x8x16 slice. The times are simulated.
512 devices in a mesh: groups: 2 (over y), section: 16 (over z), seq: 16 (over x, core).
Axes of the slice: x: 8, y: 2, z: 16, core: 2. Of those that a mesh axis runs over, the one named last changes fastest.
The devices are a block of a 8x8x16 slice.
Arguments:
- tokens: bfloat16 [8, 1024, 1440], P('groups', 'seq'), parts along dimension 0, may hold values from -6 to 6
- block_order: int32 [8], P('groups'), parts along dimension 0, may hold values from 0 to 3, each once
- prompt_lengths: int32 [8], P('groups'), parts along dimension 0, may hold values from 1 to 1024, 2304 in all
- norm_gain: float32 [16, 1440], P('section'), may hold values from 0.1 to 1.9
- w_query: bfloat16 [16, 1440, 2048], P('section', None, 'seq'), may hold values from -4 to 4
- w_key_value: bfloat16 [16, 1440, 512], P('section'), may hold values from -4 to 4
- w_out: bfloat16 [16, 2048, 1440], P('section', 'seq'), may hold values from -0.125 to 0.125
- sink_logits: float32 [16, 32], P('section'), may hold values from 0 to 4
Outputs:
- hidden_states: bfloat16 [16, 8, 1024, 1440], P('section', 'groups', 'seq'), parts along dimension 1
- layer_cache: bfloat16 [16, 8, 1024, 512], P('section', 'groups', 'seq'), parts along dimension 1
There are 2 independent parts, one for each index of `groups`. A program takes and returns all parts, laid end to end along the dimension named above; an argument that names none is the same for every part. Nothing has to cross between parts.
Inputs may be any that keep to these rules, and one draw needn't show every extreme that they name: `block_order`: each of 0 to 3 exactly once. `prompt_lengths`: the longest prompt is full.
All inputs are finite; a program needn't handle non-finite values.
Results may differ from a plain program's by a relative error of at most 0.024.
Values may be sent and summed in bfloat16 or wider, within the bound.
A program may use at most 128 MiB of HBM per device.

v0:
```python
import math
import jax
import jax.numpy as jnp
from jax import lax
from jax.sharding import PartitionSpec as P

HEAD_DIM = 64
WIN = 128
THETA = 150000.0
EPSILON = 1e-05


def rows_first(arrays, axis, dims):
    turned = [jnp.moveaxis(a, dim, 0) for a, dim in zip(arrays, dims)]
    widths = [t[0].size for t in turned]
    both = jnp.concatenate([t.reshape(-1, w) for t, w in zip(turned, widths)], axis=1)
    out = lax.all_gather(both, axis, axis=0, tiled=True)
    parts = jnp.split(out, [sum(widths[:k]) for k in range(1, len(widths))], axis=1)
    return tuple(
        (
            jnp.moveaxis(b.reshape(-1, *t.shape[1:]), 0, dim)
            for b, t, dim in zip(parts, turned, dims)
        )
    )


def from_behind(block, axis, distance):
    devices = range(lax.axis_size(axis))
    route = [(i - distance, i) for i in devices if i - distance in devices]
    return lax.ppermute(block, axis, route)


def rotary(positions, head_size):
    half = head_size // 2
    freq = jnp.exp(jnp.arange(half, dtype=jnp.float32) * (-2.0 * math.log(THETA) / head_size))
    angles = positions.astype(jnp.float32)[:, None] * freq[None, :]
    return (jnp.cos(angles)[:, None, :], jnp.sin(angles)[:, None, :])


def rotate(values, cosine, sine):
    half = values.shape[-1] // 2
    first = values[..., :half]
    second = values[..., half:]
    return jnp.concatenate([first * cosine - second * sine, second * cosine + first * sine], -1)


def per_device(
    tokens, block_order, prompt_lengths, norm_gain, w_query, w_key_value, w_out, sink_logits
):
    section_index = lax.axis_index("section")
    sections = lax.axis_size("section")
    seq_index = lax.axis_index("seq")
    micro, rows, width = tokens.shape
    full_query, full_out = rows_first((w_query, w_out), "seq", (2, 1))
    query_weight = full_query[0]
    out_weight = full_out[0]
    pair_weight = w_key_value[0]
    gain = norm_gain[0]
    heads_width = query_weight.shape[1]
    head_count = heads_width // HEAD_DIM
    kv_width = pair_weight.shape[1] // 2
    kv_heads = kv_width // HEAD_DIM
    group = head_count // kv_heads
    sink = sink_logits[0].reshape(kv_heads, group)[:, :, None]
    keep = min(WIN, rows)
    depth = WIN // keep
    start = seq_index * rows
    positions = start + jnp.arange(rows, dtype=jnp.int32)
    cosine, sine = rotary(positions, HEAD_DIM)
    key_positions = start - WIN + jnp.arange(WIN + rows, dtype=jnp.int32)

    def project(hidden):
        widened = hidden.astype(jnp.float32)
        scale = lax.rsqrt(jnp.mean(widened * widened, -1, keepdims=True) + EPSILON)
        normed = (widened * scale * gain).astype(jnp.bfloat16)
        queries = jnp.dot(normed, query_weight, preferred_element_type=jnp.float32).reshape(
            rows, head_count, HEAD_DIM
        )
        queries = rotate(queries, cosine, sine).astype(jnp.bfloat16).reshape(rows, heads_width)
        projected = jnp.dot(normed, pair_weight, preferred_element_type=jnp.float32)
        rotated = rotate(
            projected[:, :kv_width].reshape(rows, kv_heads, HEAD_DIM), cosine, sine
        ).reshape(rows, kv_width)
        cache = jnp.concatenate([rotated, projected[:, kv_width:]], 1).astype(jnp.bfloat16)
        return (queries, cache)

    def project_spare(hidden):
        return (
            jnp.zeros((rows, heads_width), jnp.bfloat16),
            jnp.zeros((rows, 2 * kv_width), jnp.bfloat16),
        )

    def window_of(cache):
        pieces = [from_behind(cache, "seq", offset) for offset in range(depth, 0, -1)]
        return jnp.concatenate(pieces, 0)

    def attend(operands):
        hidden, queries, cache, window, length = operands
        joined = jnp.concatenate([window, cache], 0)
        key_heads = joined[:, :kv_width].reshape(WIN + rows, kv_heads, HEAD_DIM)
        value_heads = joined[:, kv_width:].reshape(WIN + rows, kv_heads, HEAD_DIM)
        grouped = queries.reshape(rows, kv_heads, group, HEAD_DIM)
        scores = (
            jnp.einsum("qkgd,skd->kgqs", grouped, key_heads, preferred_element_type=jnp.float32)
            * 0.125
        )
        query_col = positions[:, None]
        key_row = key_positions[None, :]
        allowed = (key_row <= query_col) & (query_col - key_row < WIN) & (key_row >= 0)
        allowed = allowed & ((key_row < length) | (key_row == query_col))
        masked = jnp.where(allowed, scores, jnp.float32(-1e30))
        top = jnp.maximum(jnp.max(masked, -1), sink)
        expo = jnp.where(allowed, jnp.exp(scores - top[..., None]), jnp.float32(0.0))
        total = jnp.sum(expo, -1) + jnp.exp(sink - top)
        weights = (expo / total[..., None]).astype(jnp.bfloat16)
        context = jnp.einsum(
            "kgqs,skd->qkgd", weights, value_heads, preferred_element_type=jnp.float32
        )
        context = context.reshape(rows, heads_width).astype(jnp.bfloat16)
        output = jnp.dot(context, out_weight, preferred_element_type=jnp.float32)
        return (hidden.astype(jnp.float32) + output).astype(jnp.bfloat16)

    def pass_through(operands):
        return operands[0]

    def turn(counter, carry):
        arriving, hidden_buffer, cache_buffer = carry
        slot = counter - section_index
        active = (slot >= 0) & (slot < micro)
        slot_safe = jnp.clip(slot, 0, micro - 1)
        block = block_order[slot_safe]
        length = prompt_lengths[block]
        entering = lax.dynamic_index_in_dim(tokens, block, 0, keepdims=False)
        hidden = jnp.where(section_index == 0, entering, arriving)
        queries, cache = lax.cond(active, project, project_spare, hidden)
        window = window_of(cache)
        updated = lax.cond(active, attend, pass_through, (hidden, queries, cache, window, length))
        previous_hidden = lax.dynamic_index_in_dim(hidden_buffer, slot_safe, 0, keepdims=False)
        previous_cache = lax.dynamic_index_in_dim(cache_buffer, slot_safe, 0, keepdims=False)
        hidden_buffer = lax.dynamic_update_index_in_dim(
            hidden_buffer, jnp.where(active, updated, previous_hidden), slot_safe, 0
        )
        cache_buffer = lax.dynamic_update_index_in_dim(
            cache_buffer, jnp.where(active, cache, previous_cache), slot_safe, 0
        )
        passed = from_behind(updated, "section", 1)
        return (passed, hidden_buffer, cache_buffer)

    initial = (
        jnp.zeros((rows, width), jnp.bfloat16),
        jnp.zeros((micro, rows, width), jnp.bfloat16),
        jnp.zeros((micro, rows, 2 * kv_width), jnp.bfloat16),
    )
    final = lax.fori_loop(0, micro + sections - 1, turn, initial)
    return (final[1][None], final[2][None])


def solution(mesh):
    in_specs = (
        P("groups", "seq", None),
        P("groups"),
        P("groups"),
        P("section", None),
        P("section", None, "seq"),
        P("section", None, None),
        P("section", "seq", None),
        P("section", None),
    )
    out_specs = (P("section", "groups", "seq", None), P("section", "groups", "seq", None))
    return jax.shard_map(
        per_device, mesh=mesh, in_specs=in_specs, out_specs=out_specs, check_vma=False
    )
```

profile of v0, /device:TPU:1858, one launch (start us, length us, event | category | flops | bytes accessed | tf_op | source)
XLA Modules:
  0.0 783.1 jit_solution(16255271315744415141)
XLA Ops:
  10.6 83.0 %all-gather.2.cloned.1.call-done = bf16[2048,2880]{0,1:T(8,128)(2,1)} async-done(((bf16[128,2880]{0,1:T(8,128)(2,1)}), bf16[2048,2880]{0,1:T(8,128)(2,1)}) %all-gather.2.cloned.1.call-update) | async-done | bytes 11796496 | tf_op jit(solution)/shard_map/all_gather | solution.py:17
  93.6 10.2 %fusion.29 = (bf16[2048,1440]{0,1:T(8,128)(2,1)}, bf16[1440,2048]{1,0:T(8,128)(2,1)}) fusion(bf16[2048,2880]{0,1:T(8,128)(2,1)} %all-gather.2.cloned.1.call-done), kind=kLoop, calls=%fused_computation.61 | loop fusion | bytes 23592960 | tf_op jit(solution)/shard_map/split | solution.py:18
  103.8 8.7 %copy.20 = bf16[2048,1440]{1,0:T(8,128)(2,1)} copy(bf16[2048,1440]{0,1:T(8,128)(2,1)} %get-tuple-element.613) | data formatting | bytes 11796480
  114.2 662.0 %while.20 = (s32[]{:T(128)}, bf16[64,1440]{1,0:T(8,128)(2,1)S(1)}, bf16[4,64,1440]{2,1,0:T(8,128)(2,1)}, bf16[4,64,512]{2,1,0:T(8,128)(2,1)}, s32[]{:T(128)}, /*...) while((s32[]{:T(128)}, bf16[64,1440]{1,0:T(8,128)(2,1)S(1)}, ...), condition=%wide.region_8.9_spmd.clone.clone, body=%wide.region_0.8_spmd.clone.clone.sunk | while | flops 958372544 | bytes 48405112 | solution.py:154
  131.1 4.2 collective-permute-done.2
  139.3 3.4 collective-permute-start
  152.7 4.2 collective-permute-done.2
  160.9 4.0 collective-permute-start
  174.8 4.3 collective-permute-done.2
  183.1 3.7 collective-permute-start
  196.7 5.5 collective-permute-done.2
  206.1 3.2 collective-permute-start
  218.5 6.1 collective-permute-done.2
  228.6 3.2 collective-permute-start
  241.0 6.1 collective-permute-done.2
  251.2 3.2 collective-permute-start
  263.5 6.1 collective-permute-done.2
  273.7 3.2 collective-permute-start
  286.1 6.1 collective-permute-done.2
  308.6 6.1 collective-permute-done.2
  331.1 6.1 collective-permute-done.2
  353.6 6.1 collective-permute-done.2
  363.7 3.2 collective-permute-start
  376.1 6.1 collective-permute-done.2
  386.2 3.2 collective-permute-start
  398.6 6.1 collective-permute-done.2
  421.1 176.7 %collective-permute-done.2 = bf16[64,1440]{1,0:T(8,128)(2,1)S(1)} collective-permute-done((bf16[64,1440]{1,0:T(8,128)(2,1)S(1)}, bf16[64,1440]{1,0:T(8,128)(2,1)S(1)}, u32[]{:S(2)}, u32[]{:S(2)}) %collective-permute-start.2) | collective-permute-done | bytes 184352 | tf_op jit(solution)/shard_map/while/body/eval_jaxpr/ppermute | solution.py:30
  601.1 7.7 conditional.8
  603.3 3.9 fusion.26
  608.9 3.2 collective-permute-start
  618.6 7.1 conditional.9
  628.4 6.1 collective-permute-done.2
  637.8 7.7 conditional.8
  640.0 3.9 fusion.26
  645.5 3.2 collective-permute-start
  655.2 7.1 conditional.9
  665.0 6.1 collective-permute-done.2
  674.5 7.7 conditional.8
  676.6 3.9 fusion.26
  682.2 3.2 collective-permute-start
  691.9 7.1 conditional.9
  701.7 6.1 collective-permute-done.2
  711.1 7.7 conditional.8
  713.3 3.9 fusion.26
  718.8 3.2 collective-permute-start
  728.6 7.1 conditional.9
  738.3 4.9 collective-permute-done.2
  756.7 16.4 %collective-permute-start.2 = (bf16[64,1440]{1,0:T(8,128)(2,1)S(1)}, bf16[64,1440]{1,0:T(8,128)(2,1)S(1)}, u32[]{:S(2)}, u32[]{:S(2)}) collective-permute-start(bf16[64,1440]{1,0:T(8,128)(2,1)S(1)} %get-tuple-element.802), channel_id=1, source_target_pairs={{0,16},{16,32},{32,48},{48,64},{64,80},{80,96},{96,112},{112,128},... | collective-permute-start | bytes 552968 | tf_op jit(solution)/shard_map/while/body/eval_jaxpr/ppermute | solution.py:30
  (513 shorter events, 295.8 us)
Async XLA Ops:
  7.2 86.4 %all-gather.2.cloned.1.call-start = ((), (), s32[]{:S(2)}) async-start(), calls=%async_computation | async-start | bytes 12533760 | tf_op jit(solution)/shard_map/all_gather | solution.py:17
  118.3 7.8 collective-permute-start
  121.2 6.5 collective-permute-start.1
  127.7 7.6 collective-permute-start.2
  139.3 7.8 collective-permute-start
  142.8 6.5 collective-permute-start.1
  149.3 7.6 collective-permute-start.2
  160.9 8.4 %collective-permute-start = (bf16[64,512]{0,1:T(8,128)(2,1)}, bf16[64,512]{0,1:T(8,128)(2,1)S(1)}, u32[]{:S(2)}, u32[]{:S(2)}) collective-permute-start(bf16[64,512]{0,1:T(8,128)(2,1)} %get-tuple-element.727), channel_id=1, source_target_pairs={{0,2},{1,3},{2,4},{3,5},{4,6},{5,7},{6,8},{7,9},{8,10},{9,11},{10,... | collective-permute-start | bytes 196616 | tf_op jit(solution)/shard_map/while/body/eval_jaxpr/ppermute | solution.py:30
  164.9 6.5 collective-permute-start.1
  171.4 7.7 collective-permute-start.2
  183.1 8.1 %collective-permute-start = (bf16[64,512]{0,1:T(8,128)(2,1)}, bf16[64,512]{0,1:T(8,128)(2,1)S(1)}, u32[]{:S(2)}, u32[]{:S(2)}) collective-permute-start(bf16[64,512]{0,1:T(8,128)(2,1)} %get-tuple-element.727), channel_id=1, source_target_pairs={{0,2},{1,3},{2,4},{3,5},{4,6},{5,7},{6,8},{7,9},{8,10},{9,11},{10,... | collective-permute-start | bytes 196616 | tf_op jit(solution)/shard_map/while/body/eval_jaxpr/ppermute | solution.py:30
  186.8 6.5 collective-permute-start.1
  193.3 8.8 %collective-permute-start.2 = (bf16[64,1440]{1,0:T(8,128)(2,1)S(1)}, bf16[64,1440]{1,0:T(8,128)(2,1)S(1)}, u32[]{:S(2)}, u32[]{:S(2)}) collective-permute-start(bf16[64,1440]{1,0:T(8,128)(2,1)S(1)} %get-tuple-element.802), channel_id=1, source_target_pairs={{0,16},{16,32},{32,48},{48,64},{64,80},{80,96},{96,112},{112,128},... | collective-permute-start | bytes 552968 | tf_op jit(solution)/shard_map/while/body/eval_jaxpr/ppermute | solution.py:30
  206.1 7.6 collective-permute-start
  215.8 8.8 %collective-permute-start.2 = (bf16[64,1440]{1,0:T(8,128)(2,1)S(1)}, bf16[64,1440]{1,0:T(8,128)(2,1)S(1)}, u32[]{:S(2)}, u32[]{:S(2)}) collective-permute-start(bf16[64,1440]{1,0:T(8,128)(2,1)S(1)} %get-tuple-element.802), channel_id=1, source_target_pairs={{0,16},{16,32},{32,48},{48,64},{64,80},{80,96},{96,112},{112,128},... | collective-permute-start | bytes 552968 | tf_op jit(solution)/shard_map/while/body/eval_jaxpr/ppermute | solution.py:30
  228.6 7.6 collective-permute-start
  238.4 8.8 %collective-permute-start.2 = (bf16[64,1440]{1,0:T(8,128)(2,1)S(1)}, bf16[64,1440]{1,0:T(8,128)(2,1)S(1)}, u32[]{:S(2)}, u32[]{:S(2)}) collective-permute-start(bf16[64,1440]{1,0:T(8,128)(2,1)S(1)} %get-tuple-element.802), channel_id=1, source_target_pairs={{0,16},{16,32},{32,48},{48,64},{64,80},{80,96},{96,112},{112,128},... | collective-permute-start | bytes 552968 | tf_op jit(solution)/shard_map/while/body/eval_jaxpr/ppermute | solution.py:30
  251.2 7.6 collective-permute-start
  254.3 6.5 collective-permute-start.1
  260.9 8.8 %collective-permute-start.2 = (bf16[64,1440]{1,0:T(8,128)(2,1)S(1)}, bf16[64,1440]{1,0:T(8,128)(2,1)S(1)}, u32[]{:S(2)}, u32[]{:S(2)}) collective-permute-start(bf16[64,1440]{1,0:T(8,128)(2,1)S(1)} %get-tuple-element.802), channel_id=1, source_target_pairs={{0,16},{16,32},{32,48},{48,64},{64,80},{80,96},{96,112},{112,128},... | collective-permute-start | bytes 552968 | tf_op jit(solution)/shard_map/while/body/eval_jaxpr/ppermute | solution.py:30
  273.7 7.6 collective-permute-start
  276.8 6.5 collective-permute-start.1
  283.4 8.8 %collective-permute-start.2 = (bf16[64,1440]{1,0:T(8,128)(2,1)S(1)}, bf16[64,1440]{1,0:T(8,128)(2,1)S(1)}, u32[]{:S(2)}, u32[]{:S(2)}) collective-permute-start(bf16[64,1440]{1,0:T(8,128)(2,1)S(1)} %get-tuple-element.802), channel_id=1, source_target_pairs={{0,16},{16,32},{32,48},{48,64},{64,80},{80,96},{96,112},{112,128},... | collective-permute-start | bytes 552968 | tf_op jit(solution)/shard_map/while/body/eval_jaxpr/ppermute | solution.py:30
  296.2 7.6 collective-permute-start
  299.4 6.5 collective-permute-start.1
  305.9 8.8 %collective-permute-start.2 = (bf16[64,1440]{1,0:T(8,128)(2,1)S(1)}, bf16[64,1440]{1,0:T(8,128)(2,1)S(1)}, u32[]{:S(2)}, u32[]{:S(2)}) collective-permute-start(bf16[64,1440]{1,0:T(8,128)(2,1)S(1)} %get-tuple-element.802), channel_id=1, source_target_pairs={{0,16},{16,32},{32,48},{48,64},{64,80},{80,96},{96,112},{112,128},... | collective-permute-start | bytes 552968 | tf_op jit(solution)/shard_map/while/body/eval_jaxpr/ppermute | solution.py:30
  318.7 7.6 collective-permute-start
  321.9 6.5 collective-permute-start.1
  328.4 8.8 %collective-permute-start.2 = (bf16[64,1440]{1,0:T(8,128)(2,1)S(1)}, bf16[64,1440]{1,0:T(8,128)(2,1)S(1)}, u32[]{:S(2)}, u32[]{:S(2)}) collective-permute-start(bf16[64,1440]{1,0:T(8,128)(2,1)S(1)} %get-tuple-element.802), channel_id=1, source_target_pairs={{0,16},{16,32},{32,48},{48,64},{64,80},{80,96},{96,112},{112,128},... | collective-permute-start | bytes 552968 | tf_op jit(solution)/shard_map/while/body/eval_jaxpr/ppermute | solution.py:30
  341.2 7.6 collective-permute-start
  350.9 8.8 %collective-permute-start.2 = (bf16[64,1440]{1,0:T(8,128)(2,1)S(1)}, bf16[64,1440]{1,0:T(8,128)(2,1)S(1)}, u32[]{:S(2)}, u32[]{:S(2)}) collective-permute-start(bf16[64,1440]{1,0:T(8,128)(2,1)S(1)} %get-tuple-element.802), channel_id=1, source_target_pairs={{0,16},{16,32},{32,48},{48,64},{64,80},{80,96},{96,112},{112,128},... | collective-permute-start | bytes 552968 | tf_op jit(solution)/shard_map/while/body/eval_jaxpr/ppermute | solution.py:30
  363.7 7.6 collective-permute-start
  373.4 8.8 %collective-permute-start.2 = (bf16[64,1440]{1,0:T(8,128)(2,1)S(1)}, bf16[64,1440]{1,0:T(8,128)(2,1)S(1)}, u32[]{:S(2)}, u32[]{:S(2)}) collective-permute-start(bf16[64,1440]{1,0:T(8,128)(2,1)S(1)} %get-tuple-element.802), channel_id=1, source_target_pairs={{0,16},{16,32},{32,48},{48,64},{64,80},{80,96},{96,112},{112,128},... | collective-permute-start | bytes 552968 | tf_op jit(solution)/shard_map/while/body/eval_jaxpr/ppermute | solution.py:30
  386.2 7.6 collective-permute-start
  395.9 8.8 %collective-permute-start.2 = (bf16[64,1440]{1,0:T(8,128)(2,1)S(1)}, bf16[64,1440]{1,0:T(8,128)(2,1)S(1)}, u32[]{:S(2)}, u32[]{:S(2)}) collective-permute-start(bf16[64,1440]{1,0:T(8,128)(2,1)S(1)} %get-tuple-element.802), channel_id=1, source_target_pairs={{0,16},{16,32},{32,48},{48,64},{64,80},{80,96},{96,112},{112,128},... | collective-permute-start | bytes 552968 | tf_op jit(solution)/shard_map/while/body/eval_jaxpr/ppermute | solution.py:30
  408.8 7.6 collective-permute-start
  418.5 179.4 %collective-permute-start.2 = (bf16[64,1440]{1,0:T(8,128)(2,1)S(1)}, bf16[64,1440]{1,0:T(8,128)(2,1)S(1)}, u32[]{:S(2)}, u32[]{:S(2)}) collective-permute-start(bf16[64,1440]{1,0:T(8,128)(2,1)S(1)} %get-tuple-element.802), channel_id=1, source_target_pairs={{0,16},{16,32},{32,48},{48,64},{64,80},{80,96},{96,112},{112,128},... | collective-permute-start | bytes 552968 | tf_op jit(solution)/shard_map/while/body/eval_jaxpr/ppermute | solution.py:30
  608.9 7.6 collective-permute-start
  625.7 8.8 %collective-permute-start.2 = (bf16[64,1440]{1,0:T(8,128)(2,1)S(1)}, bf16[64,1440]{1,0:T(8,128)(2,1)S(1)}, u32[]{:S(2)}, u32[]{:S(2)}) collective-permute-start(bf16[64,1440]{1,0:T(8,128)(2,1)S(1)} %get-tuple-element.802), channel_id=1, source_target_pairs={{0,16},{16,32},{32,48},{48,64},{64,80},{80,96},{96,112},{112,128},... | collective-permute-start | bytes 552968 | tf_op jit(solution)/shard_map/while/body/eval_jaxpr/ppermute | solution.py:30
  645.5 7.6 collective-permute-start
  662.4 8.8 %collective-permute-start.2 = (bf16[64,1440]{1,0:T(8,128)(2,1)S(1)}, bf16[64,1440]{1,0:T(8,128)(2,1)S(1)}, u32[]{:S(2)}, u32[]{:S(2)}) collective-permute-start(bf16[64,1440]{1,0:T(8,128)(2,1)S(1)} %get-tuple-element.802), channel_id=1, source_target_pairs={{0,16},{16,32},{32,48},{48,64},{64,80},{80,96},{96,112},{112,128},... | collective-permute-start | bytes 552968 | tf_op jit(solution)/shard_map/while/body/eval_jaxpr/ppermute | solution.py:30
  682.2 7.6 collective-permute-start
  699.0 8.8 %collective-permute-start.2 = (bf16[64,1440]{1,0:T(8,128)(2,1)S(1)}, bf16[64,1440]{1,0:T(8,128)(2,1)S(1)}, u32[]{:S(2)}, u32[]{:S(2)}) collective-permute-start(bf16[64,1440]{1,0:T(8,128)(2,1)S(1)} %get-tuple-element.802), channel_id=1, source_target_pairs={{0,16},{16,32},{32,48},{48,64},{64,80},{80,96},{96,112},{112,128},... | collective-permute-start | bytes 552968 | tf_op jit(solution)/shard_map/while/body/eval_jaxpr/ppermute | solution.py:30
  718.8 7.6 collective-permute-start
  735.7 7.6 collective-permute-start.2
  747.3 7.3 collective-permute-start
  750.2 6.5 collective-permute-start.1
  756.7 19.5 %collective-permute-start.2 = (bf16[64,1440]{1,0:T(8,128)(2,1)S(1)}, bf16[64,1440]{1,0:T(8,128)(2,1)S(1)}, u32[]{:S(2)}, u32[]{:S(2)}) collective-permute-start(bf16[64,1440]{1,0:T(8,128)(2,1)S(1)} %get-tuple-element.802), channel_id=1, source_target_pairs={{0,16},{16,32},{32,48},{48,64},{64,80},{80,96},{96,112},{112,128},... | collective-permute-start | bytes 552968 | tf_op jit(solution)/shard_map/while/body/eval_jaxpr/ppermute | solution.py:30
  (31 other events, 150.7 us)
Sparse Core Ops, SparseCore 0:
  10.7 82.9 all-gather.1
where the time goes:
time: 788 us; the launch traced here: 783 us
  waiting for transfers between devices  399 us (51%)
  starting transfers between devices  153 us (19%)
  local copies, waits for them, and re-layouts  94.3 us (12%)
  other arithmetic  60.3 us (8%)
  loops' own time  34.1 us (4%)
  matrix products  28.7 us (4%)
  between operations  14.1 us (2%)
    ppermute x57, waiting for transfers between devices, from_behind(): return lax.ppermute(block, axis, route)  316 us
    ppermute x57, starting transfers between devices, from_behind(): return lax.ppermute(block, axis, route)  152 us
    all_gather x1, waiting for transfers between devices, rows_first(): out = lax.all_gather(both, axis, axis=0, tiled=True)  83 us
    another operation x1, loops' own time, per_device(): final = lax.fori_loop(0, micro + sections - 1, turn, initial)  32.9 us
    select_n x19, other arithmetic, turn(): hidden = jnp.where(section_index == 0, entering, arriving)  18.1 us
    dynamic_slice x19, local copies, waits for them, and re-layouts, turn(): lax.dynamic_index_in_dim(hidden_buffer, slot_safe, 0, keepdims=False)  18 us
    dynamic_slice x19, local copies, waits for them, and re-layouts, turn(): lax.dynamic_index_in_dim(cache_buffer, slot_safe, 0, keepdims=False)  16.2 us
  transfers between devices with their start and end apart: 58, of which 40 were waited for; matrix products, arithmetic and copies ran while one was open for 8% of the time, Pallas kernels for 0%

commit v1 on v0

--- a/solution.py
+++ b/solution.py
@@ -14,7 +14,9 @@
     turned = [jnp.moveaxis(a, dim, 0) for a, dim in zip(arrays, dims)]
     widths = [t[0].size for t in turned]
     both = jnp.concatenate([t.reshape(-1, w) for t, w in zip(turned, widths)], axis=1)
-    out = lax.all_gather(both, axis, axis=0, tiled=True)
+    out = jnp.concatenate(
+        lax.all_to_all(jnp.stack([both] * lax.axis_size(axis)), axis, 0, 0), axis=0
+    )
     parts = jnp.split(out, [sum(widths[:k]) for k in range(1, len(widths))], axis=1)
     return tuple(
         (

time: 788 us -> 997 us (1.27)
  the two profiles are of different devices: /device:TPU:1858 before, /device:TPU:1857 now
where the time goes in v1:
time: 997 us; the launch traced here: 992 us
  waiting for transfers between devices  540 us (54%)
  starting transfers between devices  214 us (21%)
  local copies, waits for them, and re-layouts  110 us (11%)
  other arithmetic  59.8 us (6%)
  loops' own time  38.5 us (4%)
  matrix products  28.8 us (3%)
    ppermute x57, waiting for transfers between devices, from_behind(): return lax.ppermute(block, axis, route)  285 us
    all_to_all x1, waiting for transfers between devices, rows_first(): lax.all_to_all(jnp.stack([both] * lax.axis_size(axis)), axis, 0, 0)  255 us
    ppermute x57, starting transfers between devices, from_behind(): return lax.ppermute(block, axis, route)  206 us
    another operation x1, loops' own time, per_device(): final = lax.fori_loop(0, micro + sections - 1, turn, initial)  37.1 us
  transfers between devices with their start and end apart: 58, of which 20 were waited for; matrix products, arithmetic and copies ran while one was open for 6% of the time, Pallas kernels for 0%

profile of v1, /device:TPU:1857, one launch (start us, length us, event | category | flops | bytes accessed | tf_op | source)
XLA Modules:
  0.0 992.1 jit_solution(12271100328495539944)
XLA Ops:
  1.8 6.6 stack.2
  8.4 8.1 all-to-all-start
  17.7 255.1 %all-to-all-done = bf16[16,128,2880]{1,2,0:T(8,128)(2,1)} async-done(((bf16[16,128,2880]{1,2,0:T(8,128)(2,1)}), bf16[16,128,2880]{1,2,0:T(8,128)(2,1)}, u32[]{:S(2)}, u32[]{:S(2)}) %all-to-all-start) | async-done | bytes 11796512 | tf_op jit(solution)/shard_map/all_to_all | solution.py:18
  272.8 6.3 copy_bitcast_fusion
  279.1 4.6 fusion.29
  283.7 8.7 copy.25
  294.1 698.0 %while.20 = (s32[]{:T(128)}, bf16[64,1440]{1,0:T(8,128)(2,1)S(1)}, bf16[4,64,1440]{2,1,0:T(8,128)(2,1)}, bf16[4,64,512]{2,1,0:T(8,128)(2,1)}, s32[]{:T(128)}, /*...) while((s32[]{:T(128)}, bf16[64,1440]{1,0:T(8,128)(2,1)S(1)}, ...), condition=%wide.region_8.9_spmd.clone.clone, body=%wide.region_0.8_spmd.clone.clone.sunk | while | flops 958372544 | bytes 48406292 | solution.py:156
  306.9 4.8 collective-permute-start.2
  320.2 4.9 collective-permute-start
  346.0 5.1 collective-permute-start.1
  353.6 4.1 collective-permute-start.2
  366.9 5.6 collective-permute-start.1
  375.0 4.1 collective-permute-start.2
  388.5 5.5 collective-permute-start.1
  409.9 5.5 collective-permute-start.1
  431.3 5.5 collective-permute-start.1
  452.8 5.5 collective-permute-start.1
  460.7 4.1 collective-permute-start.2
  474.4 5.8 collective-permute-start.1
  487.0 4.3 collective-permute-done.2
  497.0 5.8 collective-permute-start.1
  508.5 5.6 collective-permute-done.2
  519.6 5.8 collective-permute-start.1
  530.6 6.1 collective-permute-done.2
  542.3 5.8 collective-permute-start.1
  553.2 6.1 collective-permute-done.2
  564.9 5.8 collective-permute-start.1
  575.9 6.1 collective-permute-done.2
  587.5 5.8 collective-permute-start.1
  598.5 205.8 %collective-permute-done.2 = bf16[64,1440]{1,0:T(8,128)(2,1)S(1)} collective-permute-done((bf16[64,1440]{1,0:T(8,128)(2,1)S(1)}, bf16[64,1440]{1,0:T(8,128)(2,1)S(1)}, u32[]{:S(2)}, u32[]{:S(2)}) %collective-permute-start.2) | collective-permute-done | bytes 184352 | tf_op jit(solution)/shard_map/while/body/eval_jaxpr/ppermute | solution.py:32
  807.8 7.8 conditional.8
  817.0 5.7 collective-permute-start.1
  825.2 8.8 conditional.9
  836.7 6.1 collective-permute-done.2
  846.3 7.8 conditional.8
  855.4 5.7 collective-permute-start.1
  863.7 8.8 conditional.9
  875.2 6.1 collective-permute-done.2
  884.8 7.8 conditional.8
  893.9 5.7 collective-permute-start.1
  902.2 8.8 conditional.9
  913.7 6.1 collective-permute-done.2
  923.2 7.8 conditional.8
  932.4 5.7 collective-permute-start.1
  940.6 8.8 conditional.9
  952.1 4.8 collective-permute-done.2
  962.6 5.5 collective-permute-start.1
  970.6 17.8 %collective-permute-start.2 = (bf16[64,1440]{1,0:T(8,128)(2,1)S(1)}, bf16[64,1440]{1,0:T(8,128)(2,1)S(1)}, u32[]{:S(2)}, u32[]{:S(2)}) collective-permute-start(bf16[64,1440]{1,0:T(8,128)(2,1)S(1)} %get-tuple-element.831), channel_id=1, source_target_pairs={{0,16},{16,32},{32,48},{48,64},{64,80},{80,96},{96,112},{112,128},... | collective-permute-start | bytes 552968 | tf_op jit(solution)/shard_map/while/body/eval_jaxpr/ppermute | solution.py:32
  (626 shorter events, 282.9 us)
Async XLA Ops:
  8.4 264.4 %all-to-all-start = ((bf16[16,128,2880]{1,2,0:T(8,128)(2,1)}), bf16[16,128,2880]{1,2,0:T(8,128)(2,1)}, u32[]{:S(2)}, u32[]{:S(2)}) async-start(bf16[16,128,2880]{1,2,0:T(8,128)(2,1)} %stack.2), calls=%async_computation | async-start | bytes 23592960 | tf_op jit(solution)/shard_map/all_to_all | solution.py:18
  298.4 8.4 collective-permute-start
  306.9 9.1 collective-permute-start.2
  320.2 10.3 %collective-permute-start = (bf16[64,512]{0,1:T(8,128)(2,1)S(1)}, bf16[64,512]{0,1:T(8,128)(2,1)S(1)}, u32[]{:S(2)}, u32[]{:S(2)}) collective-permute-start(bf16[64,512]{0,1:T(8,128)(2,1)S(1)} %get-tuple-element.756), channel_id=1, source_target_pairs={{0,2},{1,3},{2,4},{3,5},{4,6},{5,7},{6,8},{7,9},{8,10},{9,11},{10,... | collective-permute-start | bytes 196616 | tf_op jit(solution)/shard_map/while/body/eval_jaxpr/ppermute | solution.py:32
  330.5 8.8 collective-permute-start.2
  343.7 9.9 collective-permute-start
  365.1 9.8 collective-permute-start
  366.9 8.0 collective-permute-start.1
  387.2 9.2 collective-permute-start
  388.5 7.9 collective-permute-start.1
  408.6 9.2 collective-permute-start
  409.9 7.9 collective-permute-start.1
  430.0 9.2 collective-permute-start
  431.3 7.9 collective-permute-start.1
  451.4 9.2 collective-permute-start
  460.7 8.0 collective-permute-start.2
  473.0 9.5 collective-permute-start
  474.4 8.2 collective-permute-start.1
  482.6 8.8 collective-permute-start.2
  495.7 9.5 collective-permute-start
  497.0 8.2 collective-permute-start.1
  505.3 8.8 collective-permute-start.2
  518.3 9.5 collective-permute-start
  519.6 8.2 collective-permute-start.1
  527.9 8.8 collective-permute-start.2
  540.9 9.5 collective-permute-start
  542.3 8.2 collective-permute-start.1
  550.5 8.8 collective-permute-start.2
  563.6 9.5 collective-permute-start
  564.9 8.2 collective-permute-start.1
  573.2 8.8 collective-permute-start.2
  586.2 9.5 collective-permute-start
  587.5 8.2 collective-permute-start.1
  595.8 208.5 %collective-permute-start.2 = (bf16[64,1440]{1,0:T(8,128)(2,1)S(1)}, bf16[64,1440]{1,0:T(8,128)(2,1)S(1)}, u32[]{:S(2)}, u32[]{:S(2)}) collective-permute-start(bf16[64,1440]{1,0:T(8,128)(2,1)S(1)} %get-tuple-element.831), channel_id=1, source_target_pairs={{0,16},{16,32},{32,48},{48,64},{64,80},{80,96},{96,112},{112,128},... | collective-permute-start | bytes 552968 | tf_op jit(solution)/shard_map/while/body/eval_jaxpr/ppermute | solution.py:32
  815.7 9.5 collective-permute-start
  817.0 8.2 collective-permute-start.1
  834.1 8.7 collective-permute-start.2
  854.1 9.5 collective-permute-start
  855.4 8.2 collective-permute-start.1
  872.5 8.7 collective-permute-start.2
  892.6 9.5 collective-permute-start
  893.9 8.2 collective-permute-start.1
  911.0 8.7 collective-permute-start.2
  931.1 9.5 collective-permute-start
  932.4 8.2 collective-permute-start.1
  961.3 9.2 collective-permute-start
  962.6 7.9 collective-permute-start.1
  970.6 21.5 %collective-permute-start.2 = (bf16[64,1440]{1,0:T(8,128)(2,1)S(1)}, bf16[64,1440]{1,0:T(8,128)(2,1)S(1)}, u32[]{:S(2)}, u32[]{:S(2)}) collective-permute-start(bf16[64,1440]{1,0:T(8,128)(2,1)S(1)} %get-tuple-element.831), channel_id=1, source_target_pairs={{0,16},{16,32},{32,48},{48,64},{64,80},{80,96},{96,112},{112,128},... | collective-permute-start | bytes 552968 | tf_op jit(solution)/shard_map/while/body/eval_jaxpr/ppermute | solution.py:32
  (87 other events, 1036.5 us)
